TPU v7x, 32 devices: a whole 2x2x4 slice. The times are simulated.
32 devices in a mesh: gx: 4 (over y, core), gy: 8 (over z, x).
Axes of the slice: x: 2, y: 2, z: 4, core: 2. Of those that a mesh axis runs over, the one named last changes fastest.
Arguments:
- old_master: float32 [32, 128, 1536], P('gx', 'gy'), may hold values from -3 to 3
- old_first: float32 [32, 128, 1536], P('gx', 'gy'), may hold values from -3 to 3
- old_second: float32 [32, 128, 1536], P('gx', 'gy'), may hold values from 0.01 to 1
- new_grad: bfloat16 [32, 128, 1536], P(('gx', 'gy')), may hold values from -3072 to 3072
- counts: int32 [32, 32], P(None, ('gx', 'gy')), may hold values from 1 to 72, as said below
- old_owner: int32 [32], replicated, may hold values from 0 to 31, each once
- new_owner: int32 [32], replicated, may hold values from 0 to 31, each once
Outputs:
- new_master: float32 [32, 128, 1536], P(('gx', 'gy'))
- new_first: float32 [32, 128, 1536], P(('gx', 'gy'))
- new_second: float32 [32, 128, 1536], P(('gx', 'gy'))
Inputs may be any that keep to these rules, and one draw needn't show every extreme that they name: `old_owner`: every number of 0 to 31 appears once. `new_owner`: every number of 0 to 31 appears once. `counts`: every device routed at least one token to every expert.
All inputs are finite; a program needn't handle non-finite values.
Results may differ from a plain program's by a relative error of at most 0.0003.
Values sent between devices are 32-bit elements; how exact they have to be, the bound alone decides.
A program may use at most 64 MiB of HBM per device.

v0:
```python
import jax
import jax.numpy as jnp
from jax import lax
from jax.sharding import PartitionSpec as P

first_correction = 1.0 - 0.9**10
second_correction = 1.0 - 0.999**10


def adam_step(master, first, second, grad, slot_count):
    scaled = grad.astype(jnp.float32) / slot_count
    new_first = 0.9 * first + 0.1 * scaled
    new_second = 0.999 * second + 0.001 * scaled * scaled
    step_dir = new_first / first_correction / (jnp.sqrt(new_second / second_correction) + 1e-08)
    new_master = master - 0.01 * (step_dir + 0.1 * master)
    return (new_master, new_first, new_second)


def reorder(block, groups_x, groups_y):
    total_rows = block.shape[1]
    piece = total_rows // (groups_x * groups_y)
    shaped = block.reshape(1, groups_x, groups_y, piece, block.shape[2])
    return shaped.transpose(0, 2, 1, 3, 4).reshape(1, total_rows, block.shape[2])


def body(old_master, old_first, old_second, new_grad, counts, old_owner, new_owner):
    experts = old_owner.shape[0]
    groups_x = lax.axis_size("gx")
    groups_y = lax.axis_size("gy")
    my_slot = lax.axis_index("gx") * groups_y + lax.axis_index("gy")
    slots = jnp.arange(experts, dtype=jnp.int32)
    onehot = new_owner[:, None] == slots[None, :]
    source = jnp.sum(jnp.where(onehot, old_owner[:, None], 0), axis=0)
    local_counts = counts[:, 0].astype(jnp.float32)
    by_rows = (
        lax.all_to_all(old_master, "gx", split_axis=1, concat_axis=0, tiled=True),
        lax.all_to_all(old_first, "gx", split_axis=1, concat_axis=0, tiled=True),
        lax.all_to_all(old_second, "gx", split_axis=1, concat_axis=0, tiled=True),
    )
    permuted = tuple((jnp.take(state, source, axis=0) for state in by_rows))
    landed = lax.all_to_all(permuted, ("gx", "gy"), split_axis=0, concat_axis=1, tiled=True)
    arrived = tuple((reorder(state, groups_x, groups_y) for state in landed))
    totals = lax.psum(local_counts, ("gx", "gy"))
    slot_count = jnp.sum(jnp.where(new_owner == my_slot, totals, jnp.float32(0.0)))
    return adam_step(arrived[0], arrived[1], arrived[2], new_grad, slot_count)


def solution(mesh):
    placed = (
        P("gx", "gy", None),
        P("gx", "gy", None),
        P("gx", "gy", None),
        P(("gx", "gy"), None, None),
        P(None, ("gx", "gy")),
        P(),
        P(),
    )
    return jax.shard_map(
        body,
        mesh=mesh,
        in_specs=placed,
        out_specs=(
            P(("gx", "gy"), None, None),
            P(("gx", "gy"), None, None),
            P(("gx", "gy"), None, None),
        ),
        check_vma=False,
    )
```

profile of v0, /device:TPU:0, one launch (start us, length us, event | category | flops | bytes accessed | tf_op | source)
XLA Modules:
  0.0 156.1 jit_solution(17211418162359433335)
XLA Ops:
  0.6 2.5 %copy.67 = f32[8,16,1536]{2,0,1:T(8,128)} copy(f32[8,16,1536]{2,1,0:T(8,128)} %param.9) | data formatting | bytes 1572864 | tf_op args[0]
  3.1 4.4 %all-to-all-start = ((f32[8,16,1536]{2,0,1:T(8,128)}), f32[8,16,1536]{2,0,1:T(8,128)S(1)}, u32[]{:S(2)}, u32[]{:S(2)}) async-start(f32[8,16,1536]{2,0,1:T(8,128)} %copy.67), calls=%async_computation | async-start | bytes 1572864 | tf_op jit(solution)/shard_map/all_to_all | solution.py:36
  7.5 1.3 copy.72
  8.8 10.3 %all-to-all-done = f32[8,16,1536]{2,0,1:T(8,128)S(1)} async-done(((f32[8,16,1536]{2,0,1:T(8,128)}), f32[8,16,1536]{2,0,1:T(8,128)S(1)}, u32[]{:S(2)}, u32[]{:S(2)}) %all-to-all-start) | async-done | bytes 786464 | tf_op jit(solution)/shard_map/all_to_all | solution.py:36
  19.1 3.5 %all-to-all-start.2 = ((f32[8,16,1536]{2,0,1:T(8,128)}), f32[8,16,1536]{2,0,1:T(8,128)S(1)}, u32[]{:S(2)}, u32[]{:S(2)}) async-start(f32[8,16,1536]{2,0,1:T(8,128)} %copy.72), calls=%async_computation.2 | async-start | bytes 1572864 | tf_op jit(solution)/shard_map/all_to_all | solution.py:37
  22.6 1.3 copy.78
  24.0 10.2 %all-to-all-done.2 = f32[8,16,1536]{2,0,1:T(8,128)S(1)} async-done(((f32[8,16,1536]{2,0,1:T(8,128)}), f32[8,16,1536]{2,0,1:T(8,128)S(1)}, u32[]{:S(2)}, u32[]{:S(2)}) %all-to-all-start.2) | async-done | bytes 786464 | tf_op jit(solution)/shard_map/all_to_all | solution.py:37
  34.2 3.5 %all-to-all-start.4 = ((f32[8,16,1536]{2,0,1:T(8,128)}), f32[8,16,1536]{2,0,1:T(8,128)S(1)}, u32[]{:S(2)}, u32[]{:S(2)}) async-start(f32[8,16,1536]{2,0,1:T(8,128)} %copy.78), calls=%async_computation.4 | async-start | bytes 1572864 | tf_op jit(solution)/shard_map/all_to_all | solution.py:38
  37.9 0.5 copy.69
  38.5 1.4 copy.74
  39.9 1.0 gather_fusion
  40.9 2.2 %gather_fusion.1 = f32[32,4,1536]{2,1,0:T(4,128)S(1)} fusion(f32[32,4,1536]{2,1,0:T(4,128)} %copy.74, s32[1024]{0:T(1024)S(1)} %pad_clamp_fusion), kind=kCustom, calls=%fused_computation.1.clone | custom fusion | bytes 1572992 | tf_op jit(solution)/shard_map/jit(_take)/gather | solution.py:40
  43.1 6.2 %all-to-all-done.4 = f32[8,16,1536]{2,0,1:T(8,128)S(1)} async-done(((f32[8,16,1536]{2,0,1:T(8,128)}), f32[8,16,1536]{2,0,1:T(8,128)S(1)}, u32[]{:S(2)}, u32[]{:S(2)}) %all-to-all-start.4) | async-done | bytes 786464 | tf_op jit(solution)/shard_map/all_to_all | solution.py:38
  49.9 1.0 gather_fusion.2
  50.9 1.5 broadcast_select_fusion
  52.4 27.2 %all_to_all.81 = f32[32,4,1536]{2,1,0:T(4,128)S(1)} all-to-all(f32[32,4,1536]{2,1,0:T(4,128)S(1)} %get-tuple-element.13), channel_id=1, replica_groups=mesh['gx'=4,'gy'=8] {'gx','gy'}, dimensions={0} | all-to-all | bytes 1572864 | tf_op jit(solution)/shard_map/all_to_all | solution.py:41
  79.6 24.0 %all_to_all.82 = f32[32,4,1536]{2,1,0:T(4,128)S(1)} all-to-all(f32[32,4,1536]{2,1,0:T(4,128)S(1)} %get-tuple-element.14), channel_id=1, replica_groups=mesh['gx'=4,'gy'=8] {'gx','gy'}, dimensions={0} | all-to-all | bytes 1572864 | tf_op jit(solution)/shard_map/all_to_all | solution.py:41
  103.6 2.8 %all-to-all-start.1 = ((f32[32,4,1536]{2,1,0:T(4,128)}), f32[32,4,1536]{2,1,0:T(4,128)S(1)}, u32[]{:S(2)}, u32[]{:S(2)}) async-start(f32[32,4,1536]{2,1,0:T(4,128)} %get-tuple-element.15), calls=%async_computation.1 | async-start | bytes 1572864 | tf_op jit(solution)/shard_map/all_to_all | solution.py:41
  106.4 43.1 %psum.7 = f32[32]{0:T(128)S(1)} all-reduce(f32[32]{0:T(128)S(1)} %convert_bitcast_fusion), channel_id=1, replica_groups=mesh['gx'=4,'gy'=8] {'gx','gy'}, use_global_device_ids=true, to_apply=%region_1.3 | all-reduce | flops 32 | bytes 256 | tf_op jit(solution)/shard_map/psum | solution.py:43
  149.5 0.7 fusion.3
  150.5 0.8 copy.82
  151.6 0.8 copy.76
  152.7 0.8 copy.71
  153.7 2.5 %multiply_subtract_fusion = (f32[1,128,1536]{2,1,0:T(8,128)}, f32[1,128,1536]{2,1,0:T(8,128)}, f32[1,128,1536]{2,1,0:T(8,128)}) fusion(f32[1,128,1536]{2,0,1:T(1,128)S(1)} %bitcast.45, f32[]{:T(128)} %fusion.3, bf16[1,128,1536]{2,1,0:T(8,128)(2,1)S(1)} %copy-done.2, f32[1,128,1536]{2,0,1:T(1,128)S(1)} %bitcast.44, f32[1,128,1536]{2,0,1:T(1,128)S(1)} %bitcast.43), kind=kLoop, calls=%fused_computation.14 | loop fusion | flops 2949120 | bytes 5111812 | tf_op jit(solution)/shard_map/sub | solution.py:15
  (25 shorter events, 1.8 us)
Async XLA Ops:
  3.1 4.4 %copy-start = (f32[8,16,1536]{2,1,0:T(8,128)S(1)}, f32[8,16,1536]{2,1,0:T(8,128)}, u32[]{:S(2)}) copy-start(f32[8,16,1536]{2,1,0:T(8,128)} %param.10) | copy-start | bytes 2359300
  3.1 16.0 %all-to-all-start = ((f32[8,16,1536]{2,0,1:T(8,128)}), f32[8,16,1536]{2,0,1:T(8,128)S(1)}, u32[]{:S(2)}, u32[]{:S(2)}) async-start(f32[8,16,1536]{2,0,1:T(8,128)} %copy.67), calls=%async_computation | async-start | bytes 1572864 | tf_op jit(solution)/shard_map/all_to_all | solution.py:36
  8.8 13.8 %copy-start.1 = (f32[8,16,1536]{2,1,0:T(8,128)S(1)}, f32[8,16,1536]{2,1,0:T(8,128)}, u32[]{:S(2)}) copy-start(f32[8,16,1536]{2,1,0:T(8,128)} %param.11) | copy-start | bytes 2359300
  19.1 15.1 %all-to-all-start.2 = ((f32[8,16,1536]{2,0,1:T(8,128)}), f32[8,16,1536]{2,0,1:T(8,128)S(1)}, u32[]{:S(2)}, u32[]{:S(2)}) async-start(f32[8,16,1536]{2,0,1:T(8,128)} %copy.72), calls=%async_computation.2 | async-start | bytes 1572864 | tf_op jit(solution)/shard_map/all_to_all | solution.py:37
  24.0 13.7 %copy-start.3 = (s32[32]{0:T(128)S(1)}, s32[32]{0:T(128)}, u32[]{:S(2)}) copy-start(s32[32]{0:T(128)} %param.15) | copy-start | bytes 388
  24.0 13.8 %copy-start.4 = (s32[32]{0:T(128)S(1)}, s32[32]{0:T(128)}, u32[]{:S(2)}) copy-start(s32[32]{0:T(128)} %param.14) | copy-start | bytes 388
  34.2 15.1 %all-to-all-start.4 = ((f32[8,16,1536]{2,0,1:T(8,128)}), f32[8,16,1536]{2,0,1:T(8,128)S(1)}, u32[]{:S(2)}, u32[]{:S(2)}) async-start(f32[8,16,1536]{2,0,1:T(8,128)} %copy.78), calls=%async_computation.4 | async-start | bytes 1572864 | tf_op jit(solution)/shard_map/all_to_all | solution.py:38
  103.6 2.8 %copy-start.5 = (s32[32,1]{0,1:T(1,128)S(1)}, s32[32,1]{0,1:T(1,128)}, u32[]{:S(2)}) copy-start(s32[32,1]{0,1:T(1,128)} %param.13) | copy-start | bytes 388
  103.6 48.8 %all-to-all-start.1 = ((f32[32,4,1536]{2,1,0:T(4,128)}), f32[32,4,1536]{2,1,0:T(4,128)S(1)}, u32[]{:S(2)}, u32[]{:S(2)}) async-start(f32[32,4,1536]{2,1,0:T(4,128)} %get-tuple-element.15), calls=%async_computation.1 | async-start | bytes 1572864 | tf_op jit(solution)/shard_map/all_to_all | solution.py:41
  152.7 1.0 copy-start.2
where the time goes:
time: 157 us; the launch traced here: 156 us
  blocking collectives  94.3 us (60%)
  waiting for transfers between devices  26.7 us (17%)
  local copies, waits for them, and re-layouts  14.8 us (9%)
  starting transfers between devices  14.1 us (9%)
  other arithmetic  5.31 us (3%)
    all_to_all x2, blocking collectives, body(): lax.all_to_all(permuted, ('gx', 'gy'), split_axis=0, concat_axis=1, tiled...  51.2 us
    psum x1, blocking collectives, body(): totals = lax.psum(local_counts, ('gx', 'gy'))  43.1 us
    all_to_all x1, waiting for transfers between devices, body(): lax.all_to_all(old_master, 'gx', split_axis=1, concat_axis=0, tiled=True)  10.3 us
    all_to_all x1, waiting for transfers between devices, body(): lax.all_to_all(old_first, 'gx', split_axis=1, concat_axis=0, tiled=True)  10.2 us
    all_to_all x1, waiting for transfers between devices, body(): lax.all_to_all(old_second, 'gx', split_axis=1, concat_axis=0, tiled=True)  6.23 us
    unnamed x15, local copies, waits for them, and re-layouts  5.34 us
    all_to_all x1, starting transfers between devices, body(): lax.all_to_all(old_master, 'gx', split_axis=1, concat_axis=0, tiled=True)  4.4 us
    gather x3, local copies, waits for them, and re-layouts, body(): permuted = tuple((jnp.take(state, source, axis=0) for state in by_rows))  4.19 us
  transfers between devices with their start and end apart: 4, of which 3 were waited for; matrix products, arithmetic and copies ran while one was open for 7% of the time, Pallas kernels for 0%

commit v1 on v0

--- a/solution.py
+++ b/solution.py
@@ -5,6 +5,18 @@
 
 first_correction = 1.0 - 0.9**10
 second_correction = 1.0 - 0.999**10
+
+
+def threads_serve(q_in, which_dim, work_x):
+    heard, out_arr = (q_in.shape[:which_dim], q_in.shape[which_dim + 1 :])
+    clean = q_in.reshape(*heard, work_x, -1, *out_arr)
+    return jnp.moveaxis(clean, which_dim, 0)
+
+
+def _carry_meshes(own_rows, dim_k):
+    own_rows = jnp.moveaxis(own_rows, 0, dim_k)
+    g_now = own_rows.shape
+    return own_rows.reshape(*g_now[:dim_k], g_now[dim_k] * g_now[dim_k + 1], *g_now[dim_k + 2 :])
 
 
 def adam_step(master, first, second, grad, slot_count):
@@ -32,10 +44,29 @@
     onehot = new_owner[:, None] == slots[None, :]
     source = jnp.sum(jnp.where(onehot, old_owner[:, None], 0), axis=0)
     local_counts = counts[:, 0].astype(jnp.float32)
+
+    def serve_teams(mine, ax_name, field_in, mat):
+        odd = lax.psum(1, ax_name)
+        block_last = lax.axis_index(ax_name)
+        step_out, kept_arr = (odd, block_last)
+        left_arr = threads_serve(mine, field_in, step_out)
+        steps_seen = [left_arr[kept_arr]]
+        it = 1
+        while it < step_out:
+            everything = left_arr[kept_arr ^ it]
+            outcome_arr = lax.ppermute(
+                everything, ax_name, [(ii, ii ^ it) for ii in range(step_out)]
+            )
+            steps_seen.append(outcome_arr)
+            it += 1
+        arr_now = jnp.stack(steps_seen, axis=0)
+        left_arr = arr_now[kept_arr ^ jnp.arange(step_out)]
+        return _carry_meshes(left_arr, mat)
+
     by_rows = (
         lax.all_to_all(old_master, "gx", split_axis=1, concat_axis=0, tiled=True),
         lax.all_to_all(old_first, "gx", split_axis=1, concat_axis=0, tiled=True),
-        lax.all_to_all(old_second, "gx", split_axis=1, concat_axis=0, tiled=True),
+        serve_teams(old_second, "gx", 1, 0),
     )
     permuted = tuple((jnp.take(state, source, axis=0) for state in by_rows))
     landed = lax.all_to_all(permuted, ("gx", "gy"), split_axis=0, concat_axis=1, tiled=True)

time: 157 us -> 143 us (0.911)
  waiting for transfers between devices: 26.7 us -> 15.9 us
  local copies, waits for them, and re-layouts: 14.8 us -> 12.2 us
    all_to_all x1, waiting for transfers between devices: 10.2 us -> 2.9 us  [body(): lax.all_to_all(old_first, 'gx', split_axis=1, concat_axis=0, tiled=True)]
    all_to_all x1 -> x0, waiting for transfers between devices: 6.23 us -> none  [body(): lax.all_to_all(old_second, 'gx', split_axis=1, concat_axis=0, tiled=True)]
    ppermute x0 -> x3, waiting for transfers between devices: none -> 4.88 us  [serve_teams(): lax.ppermute(everything, ax_name, [(ii, ii ^ it) for ii in range(step_out)])]
    all_to_all x1 -> x0, starting transfers between devices: 3.49 us -> none  [body(): lax.all_to_all(old_second, 'gx', split_axis=1, concat_axis=0, tiled=True)]
    ppermute x0 -> x3, starting transfers between devices: none -> 2.44 us  [serve_teams(): lax.ppermute(everything, ax_name, [(ii, ii ^ it) for ii in range(step_out)])]
    all_to_all x1, waiting for transfers between devices: 10.3 us -> 8.15 us  [body(): lax.all_to_all(old_master, 'gx', split_axis=1, concat_axis=0, tiled=True)]
    unnamed x15 -> x14, local copies, waits for them, and re-layouts: 5.34 us -> 4 us
  transfers between devices with their start and end apart: 4 -> 6, of which waited for: 3 -> 3; matrix products, arithmetic and copies ran while one was open for 7% -> 7% of each run, Pallas kernels for 0% -> 0%
where the time goes in v1:
time: 143 us
  blocking collectives  94.3 us (66%)
  waiting for transfers between devices  15.9 us (11%)
  starting transfers between devices  13.1 us (9%)
  local copies, waits for them, and re-layouts  12.2 us (9%)
  other arithmetic  6.41 us (4%)
    all_to_all x2, blocking collectives, body(): lax.all_to_all(permuted, ('gx', 'gy'), split_axis=0, concat_axis=1, tiled...  51.2 us
    psum x1, blocking collectives, body(): totals = lax.psum(local_counts, ('gx', 'gy'))  43.1 us
    all_to_all x1, waiting for transfers between devices, body(): lax.all_to_all(old_master, 'gx', split_axis=1, concat_axis=0, tiled=True)  8.15 us
    ppermute x3, waiting for transfers between devices, serve_teams(): lax.ppermute(everything, ax_name, [(ii, ii ^ it) for ii in range(step_out)])  4.88 us
    all_to_all x1, starting transfers between devices, body(): lax.all_to_all(old_master, 'gx', split_axis=1, concat_axis=0, tiled=True)  4.4 us
    unnamed x14, local copies, waits for them, and re-layouts  4 us
    all_to_all x1, starting transfers between devices, body(): lax.all_to_all(old_first, 'gx', split_axis=1, concat_axis=0, tiled=True)  3.49 us
    gather x3, local copies, waits for them, and re-layouts, body(): permuted = tuple((jnp.take(state, source, axis=0) for state in by_rows))  3.05 us
  transfers between devices with their start and end apart: 6, of which 3 were waited for; matrix products, arithmetic and copies ran while one was open for 7% of the time, Pallas kernels for 0%

profile of v1, /device:TPU:0, one launch (start us, length us, event | category | flops | bytes accessed | tf_op | source)
XLA Modules:
  0.0 142.8 jit_solution(3876921758351770140)
XLA Ops:
  0.6 2.5 %copy.58 = f32[8,16,1536]{2,0,1:T(8,128)} copy(f32[8,16,1536]{2,1,0:T(8,128)} %param.9) | data formatting | bytes 1572864 | tf_op args[0]
  3.1 4.4 %all-to-all-start = ((f32[8,16,1536]{2,0,1:T(8,128)}), f32[8,16,1536]{2,0,1:T(8,128)S(1)}, u32[]{:S(2)}, u32[]{:S(2)}) async-start(f32[8,16,1536]{2,0,1:T(8,128)} %copy.58), calls=%async_computation | async-start | bytes 1572864 | tf_op jit(solution)/shard_map/all_to_all | solution.py:67
  7.8 1.8 %collective-permute-start.2 = (f32[8,4,1536]{2,1,0:T(4,128)S(1)}, f32[8,4,1536]{2,1,0:T(4,128)S(1)}, u32[]{:S(2)}, u32[]{:S(2)}) collective-permute-start(f32[8,4,1536]{2,1,0:T(4,128)S(1)} %get-tuple-element.14), channel_id=1, source_target_pairs={{0,24},{8,16},{16,8},{24,0},{1,25},{9,17},{17,9},{25,1},{2,26},{10... | collective-permute-start | bytes 589832 | tf_op jit(solution)/shard_map/ppermute | solution.py:57
  9.6 0.6 collective-permute-start.1
  10.3 1.3 copy.63
  11.7 8.1 %all-to-all-done = f32[8,16,1536]{2,0,1:T(8,128)S(1)} async-done(((f32[8,16,1536]{2,0,1:T(8,128)}), f32[8,16,1536]{2,0,1:T(8,128)S(1)}, u32[]{:S(2)}, u32[]{:S(2)}) %all-to-all-start) | async-done | bytes 786464 | tf_op jit(solution)/shard_map/all_to_all | solution.py:67
  19.9 3.5 %all-to-all-start.2 = ((f32[8,16,1536]{2,0,1:T(8,128)}), f32[8,16,1536]{2,0,1:T(8,128)S(1)}, u32[]{:S(2)}, u32[]{:S(2)}) async-start(f32[8,16,1536]{2,0,1:T(8,128)} %copy.63), calls=%async_computation.2 | async-start | bytes 1572864 | tf_op jit(solution)/shard_map/all_to_all | solution.py:68
  23.4 4.9 %collective-permute-done.1 = f32[8,4,1536]{2,1,0:T(4,128)S(1)} collective-permute-done((f32[8,4,1536]{2,1,0:T(4,128)S(1)}, f32[8,4,1536]{2,1,0:T(4,128)S(1)}, u32[]{:S(2)}, u32[]{:S(2)}) %collective-permute-start.1) | collective-permute-done | bytes 196640 | tf_op jit(solution)/shard_map/ppermute | solution.py:57
  28.3 1.1 pad_maximum_fusion
  29.4 1.0 gather_fusion
  30.4 1.0 gather_fusion.3
  32.0 1.0 gather_fusion.1
  33.1 2.9 %all-to-all-done.2 = f32[8,16,1536]{2,0,1:T(8,128)S(1)} async-done(((f32[8,16,1536]{2,0,1:T(8,128)}), f32[8,16,1536]{2,0,1:T(8,128)S(1)}, u32[]{:S(2)}, u32[]{:S(2)}) %all-to-all-start.2) | async-done | bytes 786464 | tf_op jit(solution)/shard_map/all_to_all | solution.py:68
  36.5 1.0 gather_fusion.2
  37.6 1.5 %broadcast_select_fusion = (f32[32,4,1536]{2,1,0:T(4,128)S(1)}, f32[32,4,1536]{2,1,0:T(4,128)S(1)}, f32[32,4,1536]{2,1,0:T(4,128)}) fusion(f32[32,4,1536]{2,1,0:T(4,128)S(1)} %gather_fusion.3, pred[32]{0:T(512)(128)(4,1)S(1)} %compare_and_fusion, f32[32,4,1536]{2,1,0:T(4,128)S(1)} %gather_fusion.2, f32[32,4,1536]{2,1,0:T(4,128)S(1)} %gather_fusion.1), kind=kLoop, calls=%fused_computation.17 | loop fusion | flops 589824 | bytes 4718624 | tf_op jit(solution)/shard_map/jit(_take)/select_n | solution.py:71
  39.1 27.2 %all_to_all.63 = f32[32,4,1536]{2,1,0:T(4,128)S(1)} all-to-all(f32[32,4,1536]{2,1,0:T(4,128)S(1)} %get-tuple-element.17), channel_id=1, replica_groups=mesh['gx'=4,'gy'=8] {'gx','gy'}, dimensions={0} | all-to-all | bytes 1572864 | tf_op jit(solution)/shard_map/all_to_all | solution.py:72
  66.3 24.0 %all_to_all.64 = f32[32,4,1536]{2,1,0:T(4,128)S(1)} all-to-all(f32[32,4,1536]{2,1,0:T(4,128)S(1)} %get-tuple-element.18), channel_id=1, replica_groups=mesh['gx'=4,'gy'=8] {'gx','gy'}, dimensions={0} | all-to-all | bytes 1572864 | tf_op jit(solution)/shard_map/all_to_all | solution.py:72
  90.3 2.8 %all-to-all-start.1 = ((f32[32,4,1536]{2,1,0:T(4,128)}), f32[32,4,1536]{2,1,0:T(4,128)S(1)}, u32[]{:S(2)}, u32[]{:S(2)}) async-start(f32[32,4,1536]{2,1,0:T(4,128)} %get-tuple-element.19), calls=%async_computation.1 | async-start | bytes 1572864 | tf_op jit(solution)/shard_map/all_to_all | solution.py:72
  93.1 43.1 %psum.7 = f32[32]{0:T(128)S(1)} all-reduce(f32[32]{0:T(128)S(1)} %convert_bitcast_fusion), channel_id=1, replica_groups=mesh['gx'=4,'gy'=8] {'gx','gy'}, use_global_device_ids=true, to_apply=%region_1.3 | all-reduce | flops 32 | bytes 256 | tf_op jit(solution)/shard_map/psum | solution.py:74
  136.2 0.7 fusion.3
  137.1 0.8 copy.70
  138.2 0.8 copy.67
  139.3 0.8 copy.62
  140.3 2.4 %multiply_subtract_fusion = (f32[1,128,1536]{2,1,0:T(8,128)}, f32[1,128,1536]{2,1,0:T(8,128)}, f32[1,128,1536]{2,1,0:T(8,128)}) fusion(f32[1,128,1536]{2,0,1:T(1,128)S(1)} %bitcast.52, f32[]{:T(128)} %fusion.3, bf16[1,128,1536]{2,1,0:T(8,128)(2,1)S(1)} %copy-done.2, f32[1,128,1536]{2,0,1:T(1,128)S(1)} %bitcast.51, f32[1,128,1536]{2,0,1:T(1,128)S(1)} %bitcast.50), kind=kLoop, calls=%fused_computation.15 | loop fusion | flops 2949120 | bytes 5111812 | tf_op jit(solution)/shard_map/sub | solution.py:27
  (32 shorter events, 2.6 us)
Async XLA Ops:
  3.1 4.4 %copy-start = (f32[8,16,1536]{2,1,0:T(8,128)S(1)}, f32[8,16,1536]{2,1,0:T(8,128)}, u32[]{:S(2)}) copy-start(f32[8,16,1536]{2,1,0:T(8,128)} %param.11) | copy-start | bytes 2359300
  3.1 16.8 %all-to-all-start = ((f32[8,16,1536]{2,0,1:T(8,128)}), f32[8,16,1536]{2,0,1:T(8,128)S(1)}, u32[]{:S(2)}, u32[]{:S(2)}) async-start(f32[8,16,1536]{2,0,1:T(8,128)} %copy.58), calls=%async_computation | async-start | bytes 1572864 | tf_op jit(solution)/shard_map/all_to_all | solution.py:67
  7.7 2.5 %copy-start.1 = (f32[8,16,1536]{2,1,0:T(8,128)S(1)}, f32[8,16,1536]{2,1,0:T(8,128)}, u32[]{:S(2)}) copy-start(f32[8,16,1536]{2,1,0:T(8,128)} %param.10) | copy-start | bytes 2359300
  7.8 15.6 %collective-permute-start.2 = (f32[8,4,1536]{2,1,0:T(4,128)S(1)}, f32[8,4,1536]{2,1,0:T(4,128)S(1)}, u32[]{:S(2)}, u32[]{:S(2)}) collective-permute-start(f32[8,4,1536]{2,1,0:T(4,128)S(1)} %get-tuple-element.14), channel_id=1, source_target_pairs={{0,24},{8,16},{16,8},{24,0},{1,25},{9,17},{17,9},{25,1},{2,26},{10... | collective-permute-start | bytes 589832 | tf_op jit(solution)/shard_map/ppermute | solution.py:57
  9.6 18.7 %collective-permute-start.1 = (f32[8,4,1536]{2,1,0:T(4,128)S(1)}, f32[8,4,1536]{2,1,0:T(4,128)S(1)}, u32[]{:S(2)}, u32[]{:S(2)}) collective-permute-start(f32[8,4,1536]{2,1,0:T(4,128)S(1)} %get-tuple-element.15), channel_id=1, source_target_pairs={{0,16},{8,24},{16,0},{24,8},{1,17},{9,25},{17,1},{25,9},{2,18},{10... | collective-permute-start | bytes 589832 | tf_op jit(solution)/shard_map/ppermute | solution.py:57
  10.2 1.4 copy-start.3
  10.2 1.4 copy-start.4
  10.2 18.1 %collective-permute-start = (f32[8,4,1536]{2,1,0:T(4,128)S(1)}, f32[8,4,1536]{2,1,0:T(4,128)}, u32[]{:S(2)}, u32[]{:S(2)}) collective-permute-start(f32[8,4,1536]{2,1,0:T(4,128)S(1)} %get-tuple-element.16), channel_id=1, source_target_pairs={{0,8},{8,0},{16,24},{24,16},{1,9},{9,1},{17,25},{25,17},{2,10},{10... | collective-permute-start | bytes 589832 | tf_op jit(solution)/shard_map/ppermute | solution.py:57
  19.9 16.1 %all-to-all-start.2 = ((f32[8,16,1536]{2,0,1:T(8,128)}), f32[8,16,1536]{2,0,1:T(8,128)S(1)}, u32[]{:S(2)}, u32[]{:S(2)}) async-start(f32[8,16,1536]{2,0,1:T(8,128)} %copy.63), calls=%async_computation.2 | async-start | bytes 1572864 | tf_op jit(solution)/shard_map/all_to_all | solution.py:68
  90.3 2.8 %copy-start.5 = (s32[32,1]{0,1:T(1,128)S(1)}, s32[32,1]{0,1:T(1,128)}, u32[]{:S(2)}) copy-start(s32[32,1]{0,1:T(1,128)} %param.13) | copy-start | bytes 388
  90.3 48.7 %all-to-all-start.1 = ((f32[32,4,1536]{2,1,0:T(4,128)}), f32[32,4,1536]{2,1,0:T(4,128)S(1)}, u32[]{:S(2)}, u32[]{:S(2)}) async-start(f32[32,4,1536]{2,1,0:T(4,128)} %get-tuple-element.19), calls=%async_computation.1 | async-start | bytes 1572864 | tf_op jit(solution)/shard_map/all_to_all | solution.py:72
  139.3 1.0 copy-start.2
